TPU v7x, 32 devices: a whole 2x2x4 slice. The times are simulated.
32 devices in a mesh: dp: 8 (over z, core), mp: 4 (over y, x).
Axes of the slice: x: 2, y: 2, z: 4, core: 2. Of those that a mesh axis runs over, the one named last changes fastest.
Arguments:
- grad_parts: bfloat16 [8, 64, 256, 256], P('dp', 'mp'), may hold values from -0.25 to 0.25
- left_stats: float32 [8, 4, 4, 256, 256], P('dp', 'mp'), may hold values from -6 to 6
- right_stats: float32 [8, 4, 4, 256, 256], P('dp', 'mp'), may hold values from -6 to 6
- left_root: bfloat16 [8, 4, 4, 256, 256], P('dp', 'mp'), may hold values from -4 to 4
- right_root: bfloat16 [8, 4, 4, 256, 256], P('dp', 'mp'), may hold values from -4 to 4
- owners: int32 [64], replicated, may hold values from 0 to 3, as said below
Outputs:
- direction: bfloat16 [64, 256, 256], P('mp')
- left_updated: float32 [8, 4, 4, 256, 256], P('dp', 'mp')
- right_updated: float32 [8, 4, 4, 256, 256], P('dp', 'mp')
Inputs may be any that keep to these rules, and one draw needn't show every extreme that they name: The blocks b with the same b // 2 have distinct owners. Among the blocks of one row, no owner is named more than 4 times, and in every row some owner is named exactly 4 times.
All inputs are finite; a program needn't handle non-finite values.
Results may differ from a plain program's by a relative error of at most 0.02.
Values may be sent and summed in bfloat16 or wider, within the bound.
A program may use at most 64 MiB of HBM per device.

v0:
```python
import jax
import jax.numpy as jnp
from jax import lax
from jax.sharding import PartitionSpec as P


def per_device(grad_parts, left_stats, right_stats, left_root, right_root, owners):
    dp_count = lax.axis_size("dp")
    mp_count = lax.axis_size("mp")
    dp_index = lax.axis_index("dp")
    mp_index = lax.axis_index("mp")
    per_shard = grad_parts.shape[1]
    held_count = per_shard // dp_count
    slots_count = left_stats.shape[2]
    total_blocks = owners.shape[0]
    block_ids = jnp.arange(total_blocks, dtype=jnp.int32)
    row_of = block_ids % per_shard // held_count
    same_owner = owners[:, None] == owners[None, :]
    before = block_ids[None, :] < block_ids[:, None]
    slot_of = jnp.sum(
        ((row_of[:, None] == row_of[None, :]) & same_owner & before).astype(jnp.int32), axis=1
    )
    row_pos = jnp.arange(mp_count * held_count, dtype=jnp.int32)
    row_ids = row_pos // held_count * per_shard + dp_index * held_count + row_pos % held_count
    row_owner = jnp.take(owners, row_ids)
    row_slot = jnp.take(slot_of, row_ids)
    slot_ids = jnp.arange(slots_count, dtype=jnp.int32)
    mine_in = (row_owner[None, :] == mp_index) & (row_slot[None, :] == slot_ids[:, None])
    local_ids = (
        mp_index * per_shard + dp_index * held_count + jnp.arange(held_count, dtype=jnp.int32)
    )
    local_owner = jnp.take(owners, local_ids)
    summed = lax.psum(grad_parts[0], "dp").astype(jnp.float32)
    shares = lax.dynamic_slice_in_dim(summed, dp_index * held_count, held_count, 0)
    held_blocks = shares.astype(jnp.bfloat16)
    targets = jnp.arange(mp_count, dtype=jnp.int32)
    send_map = (local_owner[None, :] == targets[:, None]).astype(jnp.bfloat16)
    row_holder = row_pos // held_count
    receive_map = jnp.any(
        mine_in[:, :, None] & (row_holder[None, :, None] == targets[None, None, :]), axis=1
    ).astype(jnp.bfloat16)
    packed = jnp.einsum(
        "qj,jxy->qxy", send_map, held_blocks, preferred_element_type=jnp.float32
    ).astype(jnp.bfloat16)
    arrived = lax.all_to_all(packed, "mp", split_axis=0, concat_axis=0, tiled=True)
    owned_grad = jnp.einsum(
        "sq,qxy->sxy", receive_map, arrived, preferred_element_type=jnp.float32
    ).astype(jnp.bfloat16)
    left_updated = left_stats[0, 0] + jnp.einsum(
        "sik,sjk->sij", owned_grad, owned_grad, preferred_element_type=jnp.float32
    )
    right_updated = right_stats[0, 0] + jnp.einsum(
        "ski,skj->sij", owned_grad, owned_grad, preferred_element_type=jnp.float32
    )
    half_step = jnp.einsum(
        "sik,skj->sij", left_root[0, 0], owned_grad, preferred_element_type=jnp.float32
    ).astype(jnp.bfloat16)
    precond = jnp.einsum(
        "sik,skj->sij", half_step, right_root[0, 0], preferred_element_type=jnp.float32
    ).astype(jnp.bfloat16)
    out_packed = jnp.einsum(
        "sq,sxy->qxy", receive_map, precond, preferred_element_type=jnp.float32
    ).astype(jnp.bfloat16)
    came_back = lax.all_to_all(out_packed, "mp", split_axis=0, concat_axis=0, tiled=True)
    returned = jnp.einsum(
        "qj,qxy->jxy", send_map, came_back, preferred_element_type=jnp.float32
    ).astype(jnp.bfloat16)
    direction = lax.all_gather(returned, "dp", axis=0, tiled=True)
    return (direction, left_updated[None, None], right_updated[None, None])


def solution(mesh):
    in_specs = (
        P("dp", "mp", None, None),
        P("dp", "mp", None, None, None),
        P("dp", "mp", None, None, None),
        P("dp", "mp", None, None, None),
        P("dp", "mp", None, None, None),
        P(),
    )
    out_specs = (
        P("mp", None, None),
        P("dp", "mp", None, None, None),
        P("dp", "mp", None, None, None),
    )
    return jax.shard_map(
        per_device, mesh=mesh, in_specs=in_specs, out_specs=out_specs, check_vma=False
    )
```

profile of v0, /device:TPU:0, one launch (start us, length us, event | category | flops | bytes accessed | tf_op | source)
XLA Modules:
  0.0 142.9 jit_solution(12366330903584625655)
XLA Ops:
  7.2 0.0 copy-start
  7.2 0.0 all-reduce.2.cloned.1.call-start
  7.2 4.1 %copy.61 = bf16[1,16,256,256]{3,1,2,0:T(8,128)(2,1)} copy(bf16[1,16,256,256]{3,2,1,0:T(8,128)(2,1)} %param.8) | data formatting | bytes 4194304 | tf_op args[0]
  11.4 0.0 all-reduce.2.cloned.1.call-update
  11.4 0.6 copy-done.1
  12.0 0.2 convert_reduce_fusion
  12.2 0.6 gather_fusion.1
  12.9 0.6 gather_fusion.2
  13.5 0.6 gather_fusion
  14.2 65.2 %all-reduce.2.cloned.1.call-done = bf16[16,256,256]{2,0,1:T(8,128)(2,1)} async-done(((bf16[16,256,256]{2,0,1:T(8,128)(2,1)}), bf16[16,256,256]{2,0,1:T(8,128)(2,1)}) %all-reduce.2.cloned.1.call-update) | async-done | bytes 2097168 | tf_op jit(solution)/shard_map/psum | solution.py:33
  79.4 1.8 %convolution_convert_fusion.4 = bf16[4,256,256]{2,0,1:T(4,128)(2,1)S(1)} fusion(bf16[16,256,256]{2,0,1:T(8,128)(2,1)} %all-reduce.2.cloned.1.call-done, s32[]{:T(128)S(6)} %select_n.90, s32[2]{0:T(128)S(1)} %and_select_fusion.4), kind=kOutput, calls=%fused_computation.12 | convolution fusion | flops 1572872 | bytes 786444 | tf_op jit(solution)/shard_map/qj,jxy->qxy/dot_general | solution.py:42
  81.2 0.0 copy-start.3
  81.2 0.9 copy.34
  82.1 3.6 %all-to-all-start = ((bf16[4,256,256]{2,1,0:T(8,128)(2,1)}), bf16[4,256,256]{2,1,0:T(8,128)(2,1)S(1)}, u32[]{:S(2)}, u32[]{:S(2)}) async-start(bf16[4,256,256]{2,1,0:T(8,128)(2,1)} %copy.34), calls=%async_computation | async-start | bytes 1048576 | tf_op jit(solution)/shard_map/all_to_all | solution.py:45
  85.8 0.0 all-gather.2.cloned.1.call-start
  85.8 0.2 and_reduce_fusion
  85.9 6.5 %all-to-all-done = bf16[4,256,256]{2,1,0:T(8,128)(2,1)S(1)} async-done(((bf16[4,256,256]{2,1,0:T(8,128)(2,1)}), bf16[4,256,256]{2,1,0:T(8,128)(2,1)S(1)}, u32[]{:S(2)}, u32[]{:S(2)}) %all-to-all-start) | async-done | bytes 524320 | tf_op jit(solution)/shard_map/all_to_all | solution.py:45
  92.5 0.5 convolution_convert_fusion.3
  93.0 0.3 copy.36
  93.3 0.0 copy-done
  93.3 0.0 copy-done.3
  93.3 0.6 convolution_convert_fusion.1
  93.9 0.6 convolution_convert_fusion
  94.5 0.1 copy.40
  94.6 9.7 %all_to_all.10 = bf16[4,256,256]{2,1,0:T(8,128)(2,1)S(1)} all-to-all(bf16[4,256,256]{2,1,0:T(8,128)(2,1)S(1)} %copy.40), channel_id=1, replica_groups=mesh['dp'=8,'mp'=4] {'mp'}, dimensions={0} | all-to-all | bytes 1048576 | tf_op jit(solution)/shard_map/all_to_all | solution.py:64
  104.3 0.5 convolution_convert_fusion.5
  104.8 0.7 copy.42
  105.5 0.0 all-gather.2.cloned.1.call-update
  105.6 2.5 %fusion.1 = f32[1,1,4,256,256]{4,3,2,1,0:T(8,128)} fusion(f32[1,1,4,256,256]{4,3,2,1,0:T(8,128)} %param.9, bf16[4,256,256]{2,0,1:T(4,128)(2,1)S(1)} %convolution_convert_fusion.3), kind=kOutput, calls=%fused_computation.7 | convolution fusion | flops 134479872 | bytes 2621440 | tf_op jit(solution)/shard_map/sik,sjk->sij/dot_general | solution.py:49
  108.1 1.3 fusion
  109.4 23.6 %all-gather.2.cloned.1.call-done = bf16[16,256,256]{2,1,0:T(8,128)(2,1)} async-done(((bf16[2,256,256]{2,1,0:T(8,128)(2,1)}), bf16[16,256,256]{2,1,0:T(8,128)(2,1)}) %all-gather.2.cloned.1.call-update) | async-done | bytes 2097168 | tf_op jit(solution)/shard_map/all_gather | solution.py:68
  132.9 3.1 %copy.64 = bf16[16,256,256]{2,1,0:T(8,128)(2,1)} copy(bf16[16,256,256]{2,1,0:T(8,128)(2,1)} %all-gather.2.cloned.1.call-done) | data formatting | bytes 4194304
  (14 shorter events, 0.1 us)
Async XLA Ops:
  7.2 86.1 %copy-start = (bf16[1,1,4,256,256]{4,3,2,1,0:T(8,128)(2,1)S(1)}, bf16[1,1,4,256,256]{4,3,2,1,0:T(8,128)(2,1)}, u32[]{:S(2)}) copy-start(bf16[1,1,4,256,256]{4,3,2,1,0:T(8,128)(2,1)} %param.12) | copy-start | bytes 1572868
  7.2 72.2 %all-reduce.2.cloned.1.call-start = ((), (), s32[]{:S(2)}) async-start(), calls=%async_computation.2 | async-start | bytes 4194304 | tf_op jit(solution)/shard_map/psum | solution.py:33
  11.4 0.7 copy-start.1
  81.2 12.1 %copy-start.3 = (bf16[1,1,4,256,256]{4,3,2,1,0:T(8,128)(2,1)S(1)}, bf16[1,1,4,256,256]{4,3,2,1,0:T(8,128)(2,1)}, u32[]{:S(2)}) copy-start(bf16[1,1,4,256,256]{4,3,2,1,0:T(8,128)(2,1)} %param.11) | copy-start | bytes 1572868
  82.1 10.3 %all-to-all-start = ((bf16[4,256,256]{2,1,0:T(8,128)(2,1)}), bf16[4,256,256]{2,1,0:T(8,128)(2,1)S(1)}, u32[]{:S(2)}, u32[]{:S(2)}) async-start(bf16[4,256,256]{2,1,0:T(8,128)(2,1)} %copy.34), calls=%async_computation | async-start | bytes 1048576 | tf_op jit(solution)/shard_map/all_to_all | solution.py:45
  85.8 47.2 %all-gather.2.cloned.1.call-start = ((), (), s32[]{:S(2)}) async-start(), calls=%async_computation.3 | async-start | bytes 2359296 | tf_op jit(solution)/shard_map/all_gather | solution.py:68
  104.3 3.9 %copy-start.2 = (f32[1,1,4,256,256]{4,3,2,1,0:T(8,128)S(1)}, f32[1,1,4,256,256]{4,3,2,1,0:T(8,128)}, u32[]{:S(2)}) copy-start(f32[1,1,4,256,256]{4,3,2,1,0:T(8,128)} %param.10) | copy-start | bytes 3145732
Sparse Core Ops, SparseCore 0:
  11.5 67.8 all-reduce.1
  105.7 27.2 all-gather.1
where the time goes:
time: 143 us
  waiting for transfers between devices  95.3 us (67%)
  between operations  14.2 us (10%)
  local copies, waits for them, and re-layouts  11.8 us (8%)
  blocking collectives  9.67 us (7%)
  matrix products  7.86 us (5%)
  starting transfers between devices  3.69 us (3%)
    psum x1, waiting for transfers between devices, per_device(): summed = lax.psum(grad_parts[0], 'dp').astype(jnp.float32)  65.2 us
    all_gather x1, waiting for transfers between devices, per_device(): direction = lax.all_gather(returned, 'dp', axis=0, tiled=True)  23.6 us
    all_to_all x1, blocking collectives, per_device(): lax.all_to_all(out_packed, 'mp', split_axis=0, concat_axis=0, tiled=True)  9.67 us
    unnamed x10, local copies, waits for them, and re-layouts  7.84 us
    all_to_all x1, waiting for transfers between devices, per_device(): lax.all_to_all(packed, 'mp', split_axis=0, concat_axis=0, tiled=True)  6.52 us
    all_to_all x1, starting transfers between devices, per_device(): lax.all_to_all(packed, 'mp', split_axis=0, concat_axis=0, tiled=True)  3.65 us
  transfers between devices with their start and end apart: 3, of which 3 were waited for; matrix products, arithmetic and copies ran while one was open for 4% of the time, Pallas kernels for 0%

commit v1 on v0

--- a/solution.py
+++ b/solution.py
@@ -30,7 +30,7 @@
         mp_index * per_shard + dp_index * held_count + jnp.arange(held_count, dtype=jnp.int32)
     )
     local_owner = jnp.take(owners, local_ids)
-    summed = lax.psum(grad_parts[0], "dp").astype(jnp.float32)
+    summed = jnp.sum(lax.all_gather(grad_parts[0], "dp"), axis=0).astype(jnp.float32)
     shares = lax.dynamic_slice_in_dim(summed, dp_index * held_count, held_count, 0)
     held_blocks = shares.astype(jnp.bfloat16)
     targets = jnp.arange(mp_count, dtype=jnp.int32)

time: 143 us -> 237 us (1.66)
  waiting for transfers between devices: 95.3 us -> 185 us
  other arithmetic: 0.42 us -> 9.57 us
  local copies, waits for them, and re-layouts: 11.8 us -> 7.07 us
    all_gather x0 -> x1, waiting for transfers between devices: none -> 153 us  [per_device(): lax.all_gather(grad_parts[0], 'dp')]
    psum x1 -> x0, waiting for transfers between devices: 65.2 us -> none  [per_device(): summed = lax.psum(grad_parts[0], 'dp').astype(jnp.float32)]
    reduce_sum x0 -> x1, other arithmetic: none -> 9.14 us  [per_device(): jnp.sum(lax.all_gather(grad_parts[0], 'dp'), axis=0).astype(jnp.float32)]
    unnamed x10 -> x9, local copies, waits for them, and re-layouts: 7.84 us -> 3.12 us
  transfers between devices with their start and end apart: 3 -> 3, of which waited for: 3 -> 3; matrix products, arithmetic and copies ran while one was open for 4% -> 3% of each run, Pallas kernels for 0% -> 0%
where the time goes in v1:
time: 237 us; the launch traced here: 236 us
  waiting for transfers between devices  185 us (78%)
  between operations  14.2 us (6%)
  blocking collectives  10.6 us (4%)
  other arithmetic  9.57 us (4%)
  local copies, waits for them, and re-layouts  7.07 us (3%)
  matrix products  6.63 us (3%)
  starting transfers between devices  3.69 us (2%)
    all_gather x1, waiting for transfers between devices, per_device(): lax.all_gather(grad_parts[0], 'dp')  153 us
    all_gather x1, waiting for transfers between devices, per_device(): direction = lax.all_gather(returned, 'dp', axis=0, tiled=True)  22.2 us
    all_to_all x1, blocking collectives, per_device(): lax.all_to_all(out_packed, 'mp', split_axis=0, concat_axis=0, tiled=True)  10.6 us
    reduce_sum x1, other arithmetic, per_device(): jnp.sum(lax.all_gather(grad_parts[0], 'dp'), axis=0).astype(jnp.float32)  9.14 us
    all_to_all x1, waiting for transfers between devices, per_device(): lax.all_to_all(packed, 'mp', split_axis=0, concat_axis=0, tiled=True)  8.33 us
  transfers between devices with their start and end apart: 3, of which 3 were waited for; matrix products, arithmetic and copies ran while one was open for 3% of the time, Pallas kernels for 0%

profile of v1, /device:TPU:0, one launch (start us, length us, event | category | flops | bytes accessed | tf_op | source)
XLA Modules:
  0.0 236.2 jit_solution(12910935962060760346)
XLA Ops:
  7.2 0.0 copy-start
  7.2 0.0 copy-start.1
  7.2 0.0 all-gather.3.cloned.1.call-start
  7.2 0.7 all-gather.3.cloned.1.call-update
  8.0 0.0 copy-done.1
  8.0 0.6 gather_fusion
  8.6 0.6 gather_fusion.1
  9.3 0.2 convert_reduce_fusion
  9.5 0.6 gather_fusion.2
  10.2 153.3 %all-gather.3.cloned.1.call-done = bf16[8,16,256,256]{3,2,1,0:T(8,128)(2,1)} async-done(((bf16[1,16,256,256]{3,2,1,0:T(8,128)(2,1)}), bf16[8,16,256,256]{3,2,1,0:T(8,128)(2,1)}) %all-gather.3.cloned.1.call-update) | async-done | bytes 16777232 | tf_op jit(solution)/shard_map/all_gather | solution.py:33
  163.4 9.1 %reduce_sum.22 = bf16[16,256,256]{2,1,0:T(8,128)(2,1)S(1)} reduce(bf16[8,16,256,256]{3,2,1,0:T(8,128)(2,1)} %all-gather.3.cloned.1.call-done, bf16[]{:T(256)} %constant.100.clone.1), dimensions={0}, to_apply=%region_2.4 | reduce | flops 7340032 | bytes 18874370 | tf_op jit(solution)/shard_map/reduce_sum | solution.py:33
  172.6 0.6 convolution_convert_fusion.4
  173.2 0.0 copy-start.3
  173.2 0.9 copy.47
  174.1 3.6 %all-to-all-start = ((bf16[4,256,256]{2,1,0:T(8,128)(2,1)}), bf16[4,256,256]{2,1,0:T(8,128)(2,1)S(1)}, u32[]{:S(2)}, u32[]{:S(2)}) async-start(bf16[4,256,256]{2,1,0:T(8,128)(2,1)} %copy.47), calls=%async_computation | async-start | bytes 1048576 | tf_op jit(solution)/shard_map/all_to_all | solution.py:45
  177.8 0.2 and_reduce_fusion
  177.9 8.3 %all-to-all-done = bf16[4,256,256]{2,1,0:T(8,128)(2,1)S(1)} async-done(((bf16[4,256,256]{2,1,0:T(8,128)(2,1)}), bf16[4,256,256]{2,1,0:T(8,128)(2,1)S(1)}, u32[]{:S(2)}, u32[]{:S(2)}) %all-to-all-start) | async-done | bytes 524320 | tf_op jit(solution)/shard_map/all_to_all | solution.py:45
  186.2 0.5 convolution_convert_fusion.3
  186.8 0.3 copy.49
  187.1 0.0 copy-done
  187.1 0.0 copy-done.3
  187.1 0.6 convolution_convert_fusion.1
  187.7 0.6 convolution_convert_fusion
  188.3 0.1 copy.53
  188.4 10.6 %all_to_all.10 = bf16[4,256,256]{2,1,0:T(8,128)(2,1)S(1)} all-to-all(bf16[4,256,256]{2,1,0:T(8,128)(2,1)S(1)} %copy.53), channel_id=1, replica_groups=mesh['dp'=8,'mp'=4] {'mp'}, dimensions={0} | all-to-all | bytes 1048576 | tf_op jit(solution)/shard_map/all_to_all | solution.py:64
  198.9 0.5 convolution_convert_fusion.5
  199.5 0.7 copy.55
  200.2 0.0 all-gather.5.cloned.1.call-update
  200.2 2.5 %fusion.1 = f32[1,1,4,256,256]{4,3,2,1,0:T(8,128)} fusion(f32[1,1,4,256,256]{4,3,2,1,0:T(8,128)} %param.9, bf16[4,256,256]{2,0,1:T(4,128)(2,1)S(1)} %convolution_convert_fusion.3), kind=kOutput, calls=%fused_computation.6 | convolution fusion | flops 134479872 | bytes 2621440 | tf_op jit(solution)/shard_map/sik,sjk->sij/dot_general | solution.py:49
  202.8 1.3 fusion
  204.1 22.2 %all-gather.5.cloned.1.call-done = bf16[16,256,256]{2,1,0:T(8,128)(2,1)} async-done(((bf16[2,256,256]{2,1,0:T(8,128)(2,1)}), bf16[16,256,256]{2,1,0:T(8,128)(2,1)}) %all-gather.5.cloned.1.call-update) | async-done | bytes 2097168 | tf_op jit(solution)/shard_map/all_gather | solution.py:68
  226.3 3.1 %copy.79 = bf16[16,256,256]{2,1,0:T(8,128)(2,1)} copy(bf16[16,256,256]{2,1,0:T(8,128)(2,1)} %all-gather.5.cloned.1.call-done) | data formatting | bytes 4194304
  (15 shorter events, 0.1 us)
Async XLA Ops:
  7.2 179.9 %copy-start = (bf16[1,1,4,256,256]{4,3,2,1,0:T(8,128)(2,1)S(1)}, bf16[1,1,4,256,256]{4,3,2,1,0:T(8,128)(2,1)}, u32[]{:S(2)}) copy-start(bf16[1,1,4,256,256]{4,3,2,1,0:T(8,128)(2,1)} %param.12) | copy-start | bytes 1572868
  7.2 0.8 copy-start.1
  7.2 156.2 %all-gather.3.cloned.1.call-start = ((), (), s32[]{:S(2)}) async-start(), calls=%async_computation.2 | async-start | bytes 18874368 | tf_op jit(solution)/shard_map/all_gather | solution.py:33
  173.2 13.9 %copy-start.3 = (bf16[1,1,4,256,256]{4,3,2,1,0:T(8,128)(2,1)S(1)}, bf16[1,1,4,256,256]{4,3,2,1,0:T(8,128)(2,1)}, u32[]{:S(2)}) copy-start(bf16[1,1,4,256,256]{4,3,2,1,0:T(8,128)(2,1)} %param.11) | copy-start | bytes 1572868
  174.1 12.2 %all-to-all-start = ((bf16[4,256,256]{2,1,0:T(8,128)(2,1)}), bf16[4,256,256]{2,1,0:T(8,128)(2,1)S(1)}, u32[]{:S(2)}, u32[]{:S(2)}) async-start(bf16[4,256,256]{2,1,0:T(8,128)(2,1)} %copy.47), calls=%async_computation | async-start | bytes 1048576 | tf_op jit(solution)/shard_map/all_to_all | solution.py:45
  177.7 48.5 %all-gather.5.cloned.1.call-start = ((), (), s32[]{:S(2)}) async-start(), calls=%async_computation.3 | async-start | bytes 2359296 | tf_op jit(solution)/shard_map/all_gather | solution.py:68
  198.9 3.9 %copy-start.2 = (f32[1,1,4,256,256]{4,3,2,1,0:T(8,128)S(1)}, f32[1,1,4,256,256]{4,3,2,1,0:T(8,128)}, u32[]{:S(2)}) copy-start(f32[1,1,4,256,256]{4,3,2,1,0:T(8,128)} %param.10) | copy-start | bytes 3145732
Sparse Core Ops, SparseCore 0:
  9.6 153.7 all-gather.2
  200.4 25.8 all-gather.4
